TPU v7x, 32 devices: a whole 2x2x4 slice. The times are simulated.
32 devices in a mesh: row: 8 (over z, y), ta: 4 (over x, core).
Axes of the slice: x: 2, y: 2, z: 4, core: 2. Of those that a mesh axis runs over, the one named last changes fastest.
Arguments:
- hidden: bfloat16 [8, 256, 3584], P('row', None, 'ta'), may hold values from -6 to 6
- target: bfloat16 [8, 256, 3584], P('row', None, 'ta'), may hold values from -6 to 6
- w_down: bfloat16 [8, 2, 3584, 256], P('row', None, 'ta'), may hold values from -5 to 5
- w_up: bfloat16 [8, 2, 256, 3584], P('row', None, None, 'ta'), may hold values from -5 to 5
- m_down: float32 [8, 2, 3584, 256], P('row', None, 'ta'), may hold values from -9 to 9
- m_up: float32 [8, 2, 256, 3584], P('row', None, None, 'ta'), may hold values from -9 to 9
Outputs:
- avg_down: bfloat16 [2, 3584, 256], P(None, 'ta')
- avg_up: bfloat16 [2, 256, 3584], P(None, None, 'ta')
- mom_down: float32 [2, 3584, 256], P(None, 'ta')
- mom_up: float32 [2, 256, 3584], P(None, None, 'ta')
All inputs are finite; a program needn't handle non-finite values.
Results may differ from a plain program's by a relative error of at most 0.019.
Values may be sent and summed in bfloat16 or wider, within the bound.
No kernel may reach another device: no remote copies, remote signals or barrier semaphores. Data moves between devices by JAX's collectives and lax.ppermute only.
A program may use at most 128 MiB of HBM per device.

v0:
```python
import jax
import jax.numpy as jnp
from jax import lax
from jax.sharding import PartitionSpec as P

D = 3584
RANK = 256
STEPS = 4
norm_eps = 1e-06
learn_rate = 0.02
moment_decay = 0.9


def contract(matrix_a, matrix_b, dim_a, dim_b):
    return lax.dot_general(
        matrix_a, matrix_b, (((dim_a,), (dim_b,)), ((), ())), preferred_element_type=jnp.float32
    )


def silu_slope(preact):
    sigmoid_v = jax.nn.sigmoid(preact)
    return sigmoid_v * (1.0 + preact * (1.0 - sigmoid_v))


def forward_layer(hidden, weights):
    w_down, w_up = weights
    wide_rows = hidden.astype(jnp.float32)
    squares = jnp.sum(wide_rows * wide_rows, axis=1)
    partial_value = jnp.dot(hidden, w_down, preferred_element_type=jnp.float32) * D ** (-0.5)
    projected, total_sq = lax.psum((partial_value, squares), "ta")
    root_mean = jnp.sqrt(total_sq / D + norm_eps)[:, None]
    preact = projected / root_mean
    activation = jax.nn.silu(preact).astype(jnp.bfloat16)
    lifted = jnp.dot(activation, w_up, preferred_element_type=jnp.float32) * RANK ** (-0.5)
    outcome = (wide_rows + lifted).astype(jnp.bfloat16)
    return (outcome, (hidden, root_mean, preact, activation))


def backward_layer(gradient, inputs):
    stored, weights, moments = inputs
    hidden, root_mean, preact, activation = stored
    w_down, w_up = weights
    grad_low = gradient.astype(jnp.bfloat16)
    grad_up = contract(activation, grad_low, 0, 0) * RANK ** (-0.5)
    grad_act = lax.psum(
        (contract(grad_low, w_up, 1, 1) * RANK ** (-0.5)).astype(jnp.bfloat16), "ta"
    ).astype(jnp.float32)
    grad_pre = grad_act * silu_slope(preact)
    row_dot = jnp.sum(grad_pre * preact, axis=1, keepdims=True)
    grad_proj = (grad_pre / root_mean).astype(jnp.bfloat16)
    grad_down = contract(hidden, grad_proj, 0, 0) * D ** (-0.5)
    wide_rows = hidden.astype(jnp.float32)
    through = contract(grad_proj, w_down, 1, 1) * D ** (-0.5)
    gradient = gradient + through - row_dot * wide_rows / (D * root_mean * root_mean)
    moment_down = moment_decay * moments[0] + grad_down
    moment_up = moment_decay * moments[1] + grad_up
    new_down = (w_down.astype(jnp.float32) - learn_rate * moment_down).astype(jnp.bfloat16)
    new_up = (w_up.astype(jnp.float32) - learn_rate * moment_up).astype(jnp.bfloat16)
    return (gradient, (new_down, new_up, moment_down, moment_up))


def average_whole(states):
    replicas = lax.axis_size("row")
    flat_down = states[0].astype(jnp.float32).reshape(-1)
    flat_up = states[1].astype(jnp.float32).reshape(-1)
    flat_mdown = states[2].reshape(-1)
    flat_mup = states[3].reshape(-1)
    totals = (
        lax.psum_scatter(flat_down, "row", scatter_dimension=0, tiled=True),
        lax.psum_scatter(flat_up, "row", scatter_dimension=0, tiled=True),
        lax.psum_scatter(flat_mdown, "row", scatter_dimension=0, tiled=True),
        lax.psum_scatter(flat_mup, "row", scatter_dimension=0, tiled=True),
    )
    share_down = (totals[0] / replicas).astype(jnp.bfloat16)
    share_up = (totals[1] / replicas).astype(jnp.bfloat16)
    params = (
        lax.all_gather(share_down, "row", axis=0, tiled=True),
        lax.all_gather(share_up, "row", axis=0, tiled=True),
    )
    moments = (
        lax.all_gather(
            (totals[2] / replicas).astype(jnp.bfloat16), "row", axis=0, tiled=True
        ).astype(jnp.float32),
        lax.all_gather(
            (totals[3] / replicas).astype(jnp.bfloat16), "row", axis=0, tiled=True
        ).astype(jnp.float32),
    )
    return (
        params[0].reshape(states[0].shape),
        params[1].reshape(states[1].shape),
        moments[0].reshape(states[2].shape),
        moments[1].reshape(states[3].shape),
    )


def body(hidden, target, w_down, w_up, m_down, m_up):
    tokens = hidden[0]
    target_rows = target[0].astype(jnp.float32)
    states = (w_down[0], w_up[0], m_down[0], m_up[0])
    for step_index in range(STEPS):
        outcome, stored = lax.scan(forward_layer, tokens, (states[0], states[1]))
        gradient = outcome.astype(jnp.float32) - target_rows
        gradient, states = lax.scan(
            backward_layer,
            gradient,
            (stored, (states[0], states[1]), (states[2], states[3])),
            reverse=True,
        )
    states = average_whole(states)
    return (states[0], states[1], states[2], states[3])


def solution(mesh):
    placed = (
        P("row", None, "ta"),
        P("row", None, "ta"),
        P("row", None, "ta", None),
        P("row", None, None, "ta"),
        P("row", None, "ta", None),
        P("row", None, None, "ta"),
    )
    return jax.shard_map(
        body,
        mesh=mesh,
        in_specs=placed,
        out_specs=(
            P(None, "ta", None),
            P(None, None, "ta"),
            P(None, "ta", None),
            P(None, None, "ta"),
        ),
        check_vma=False,
    )
```

profile of v0, /device:TPU:0, one launch (start us, length us, event | category | flops | bytes accessed | tf_op | source)
XLA Modules:
  0.0 1070.3 jit_solution(8603271068688036088)
XLA Ops:
  11.1 83.1 %while.160 = (s32[]{:T(128)}, bf16[256,896]{1,0:T(8,128)(2,1)S(1)}, bf16[2,256,896]{2,1,0:T(8,128)(2,1)}, f32[2,256,1]{1,2,0:T(1,128)S(1)}, f32[2,256,256]{1,2,0...) while((s32[]{:T(128)}, bf16[256,896]{1,0:T(8,128)(2,1)S(1)}, ...), condition=%wide.region_4.5_spmd, body=%wide.region_0.4_spmd.sunk | while | flops 237470208 | bytes 6695077 | solution.py:101
  22.6 27.2 %all-reduce.17.cloned.1.call-done = f32[256,256]{0,1:T(8,128)} async-done(((f32[256,256]{0,1:T(8,128)}), f32[256,256]{0,1:T(8,128)}) %all-reduce.17.cloned.1.call-update) | async-done | bytes 262160 | tf_op jit(solution)/shard_map/while/body/eval_jaxpr/psum | solution.py:30
  62.9 27.1 %all-reduce.17.cloned.1.call-done = f32[256,256]{0,1:T(8,128)} async-done(((f32[256,256]{0,1:T(8,128)}), f32[256,256]{0,1:T(8,128)}) %all-reduce.17.cloned.1.call-update) | async-done | bytes 262160 | tf_op jit(solution)/shard_map/while/body/eval_jaxpr/psum | solution.py:30
  98.1 80.0 %while.161 = (s32[]{:T(128)}, f32[256,896]{1,0:T(8,128)S(1)}, bf16[2,896,256]{2,1,0:T(8,128)(2,1)}, bf16[2,256,896]{2,1,0:T(8,128)(2,1)S(1)}, f32[2,896,256]{2,1...) while((s32[]{:T(128)}, f32[256,896]{1,0:T(8,128)S(1)}, ...), condition=%wide.region_8.9_spmd, body=%wide.region_5.8_spmd.sunk | while | flops 477167872 | bytes 56243636 | solution.py:103
  103.3 29.7 %all-reduce.19.cloned.1.call-done = bf16[256,256]{0,1:T(8,128)(2,1)} async-done(((bf16[256,256]{0,1:T(8,128)(2,1)}), bf16[256,256]{0,1:T(8,128)(2,1)}) %all-reduce.19.cloned.1.call-update) | async-done | bytes 131088 | tf_op jit(solution)/shard_map/while/body/eval_jaxpr/psum | solution.py:45
  143.5 29.3 %all-reduce.19.cloned.1.call-done = bf16[256,256]{0,1:T(8,128)(2,1)} async-done(((bf16[256,256]{0,1:T(8,128)(2,1)}), bf16[256,256]{0,1:T(8,128)(2,1)}) %all-reduce.19.cloned.1.call-update) | async-done | bytes 131088 | tf_op jit(solution)/shard_map/while/body/eval_jaxpr/psum | solution.py:45
  179.2 77.3 %while.162 = (s32[]{:T(128)}, bf16[256,896]{1,0:T(8,128)(2,1)S(1)}, bf16[2,256,896]{2,1,0:T(8,128)(2,1)}, f32[2,256,1]{1,2,0:T(1,128)S(1)}, f32[2,256,256]{1,2,0...) while((s32[]{:T(128)}, bf16[256,896]{1,0:T(8,128)(2,1)S(1)}, ...), condition=%wide.region_13.14_spmd, body=%wide.region_9.13_spmd.sunk | while | flops 237470208 | bytes 6695077 | solution.py:101
  263.1 80.4 %while.163 = (s32[]{:T(128)}, f32[256,896]{1,0:T(8,128)S(1)}, bf16[2,896,256]{2,1,0:T(8,128)(2,1)}, bf16[2,256,896]{2,1,0:T(8,128)(2,1)}, f32[2,896,256]{2,1,0:T...) while((s32[]{:T(128)}, f32[256,896]{1,0:T(8,128)S(1)}, ...), condition=%wide.region_17.18_spmd, body=%wide.region_14.17_spmd.sunk | while | flops 477167872 | bytes 56243636 | solution.py:103
  267.9 30.1 %all-reduce.23.cloned.1.call-done = bf16[256,256]{0,1:T(8,128)(2,1)} async-done(((bf16[256,256]{0,1:T(8,128)(2,1)}), bf16[256,256]{0,1:T(8,128)(2,1)}) %all-reduce.23.cloned.1.call-update) | async-done | bytes 131088 | tf_op jit(solution)/shard_map/while/body/eval_jaxpr/psum | solution.py:45
  308.1 30.1 %all-reduce.23.cloned.1.call-done = bf16[256,256]{0,1:T(8,128)(2,1)} async-done(((bf16[256,256]{0,1:T(8,128)(2,1)}), bf16[256,256]{0,1:T(8,128)(2,1)}) %all-reduce.23.cloned.1.call-update) | async-done | bytes 131088 | tf_op jit(solution)/shard_map/while/body/eval_jaxpr/psum | solution.py:45
  344.5 78.8 %while.164 = (s32[]{:T(128)}, bf16[256,896]{1,0:T(8,128)(2,1)S(1)}, bf16[2,256,896]{2,1,0:T(8,128)(2,1)}, f32[2,256,1]{1,2,0:T(1,128)S(1)}, f32[2,256,256]{1,2,0...) while((s32[]{:T(128)}, bf16[256,896]{1,0:T(8,128)(2,1)S(1)}, ...), condition=%wide.region_22.23_spmd, body=%wide.region_18.22_spmd.sunk | while | flops 237470208 | bytes 10365121 | solution.py:101
  353.5 27.0 %all-reduce.25.cloned.1.call-done = f32[256,256]{0,1:T(8,128)} async-done(((f32[256,256]{0,1:T(8,128)}), f32[256,256]{0,1:T(8,128)}) %all-reduce.25.cloned.1.call-update) | async-done | bytes 262160 | tf_op jit(solution)/shard_map/while/body/eval_jaxpr/psum | solution.py:30
  428.8 80.1 %while.165 = (s32[]{:T(128)}, f32[256,896]{1,0:T(8,128)S(1)}, bf16[2,896,256]{2,1,0:T(8,128)(2,1)}, bf16[2,256,896]{2,1,0:T(8,128)(2,1)}, f32[2,896,256]{2,1,0:T...) while((s32[]{:T(128)}, f32[256,896]{1,0:T(8,128)S(1)}, ...), condition=%wide.region_26.27_spmd, body=%wide.region_23.26_spmd.sunk | while | flops 477167872 | bytes 56243636 | solution.py:103
  433.6 30.1 %all-reduce.27.cloned.1.call-done = bf16[256,256]{0,1:T(8,128)(2,1)} async-done(((bf16[256,256]{0,1:T(8,128)(2,1)}), bf16[256,256]{0,1:T(8,128)(2,1)}) %all-reduce.27.cloned.1.call-update) | async-done | bytes 131088 | tf_op jit(solution)/shard_map/while/body/eval_jaxpr/psum | solution.py:45
  473.8 29.8 %all-reduce.27.cloned.1.call-done = bf16[256,256]{0,1:T(8,128)(2,1)} async-done(((bf16[256,256]{0,1:T(8,128)(2,1)}), bf16[256,256]{0,1:T(8,128)(2,1)}) %all-reduce.27.cloned.1.call-update) | async-done | bytes 131088 | tf_op jit(solution)/shard_map/while/body/eval_jaxpr/psum | solution.py:45
  509.9 77.6 %while.166 = (s32[]{:T(128)}, bf16[256,896]{1,0:T(8,128)(2,1)S(1)}, bf16[2,256,896]{2,1,0:T(8,128)(2,1)}, f32[2,256,1]{1,2,0:T(1,128)S(1)}, f32[2,256,256]{1,2,0...) while((s32[]{:T(128)}, bf16[256,896]{1,0:T(8,128)(2,1)S(1)}, ...), condition=%wide.region_31.32_spmd, body=%wide.region_27.31_spmd.sunk | while | flops 237470208 | bytes 10365121 | solution.py:101
  593.0 80.6 %while.167 = (s32[]{:T(128)}, f32[256,896]{1,0:T(8,128)S(1)}, bf16[2,896,256]{2,1,0:T(8,128)(2,1)}, bf16[2,256,896]{2,1,0:T(8,128)(2,1)}, f32[2,896,256]{2,1,0:T...) while((s32[]{:T(128)}, f32[256,896]{1,0:T(8,128)S(1)}, ...), condition=%wide.region_35.36_spmd, body=%wide.region_32.35_spmd.sunk | while | flops 477167872 | bytes 52573592 | solution.py:103
  597.8 30.4 %all-reduce.31.cloned.1.call-done = bf16[256,256]{0,1:T(8,128)(2,1)} async-done(((bf16[256,256]{0,1:T(8,128)(2,1)}), bf16[256,256]{0,1:T(8,128)(2,1)}) %all-reduce.31.cloned.1.call-update) | async-done | bytes 131088 | tf_op jit(solution)/shard_map/while/body/eval_jaxpr/psum | solution.py:45
  638.1 30.4 %all-reduce.31.cloned.1.call-done = bf16[256,256]{0,1:T(8,128)(2,1)} async-done(((bf16[256,256]{0,1:T(8,128)(2,1)}), bf16[256,256]{0,1:T(8,128)(2,1)}) %all-reduce.31.cloned.1.call-update) | async-done | bytes 131088 | tf_op jit(solution)/shard_map/while/body/eval_jaxpr/psum | solution.py:45
  685.9 237.4 %all-reduce.15.cloned.1.call-done = (f32[458752]{0:T(1024)}, f32[458752]{0:T(1024)}, f32[458752]{0:T(1024)}, f32[458752]{0:T(1024)}) async-done(((f32[458752]{0:T(1024)}, f32[458752]{0:T(1024)}, f32[458752]{0:T(1024)}, f32[458752]{0:T(1024)}), (f32[458752]{0:T(1024)}, f32[458752]{0:T(1024)}, f32[458752]{0:T(1024)}, f32[458752]{0:T(1024)})) %all-reduce.15.cloned.1.call-update) | async-done | bytes 7340048
  924.3 32.4 %all_gather.14 = bf16[458752]{0:T(1024)(128)(2,1)S(1)} all-gather(bf16[57344]{0:T(1024)(128)(2,1)S(1)} %fusion.173), channel_id=1, replica_groups=mesh['row'=8,'ta'=4] {'row'}, dimensions={0}, use_global_device_ids=true | all-gather | bytes 1032192 | tf_op jit(solution)/shard_map/all_gather | solution.py:81
  959.1 32.4 %all_gather.15 = bf16[458752]{0:T(1024)(128)(2,1)S(1)} all-gather(bf16[57344]{0:T(1024)(128)(2,1)S(1)} %fusion.172), channel_id=1, replica_groups=mesh['row'=8,'ta'=4] {'row'}, dimensions={0}, use_global_device_ids=true | all-gather | bytes 1032192 | tf_op jit(solution)/shard_map/all_gather | solution.py:84
  994.5 32.7 %all_gather.12 = bf16[458752]{0:T(1024)(128)(2,1)S(1)} all-gather(bf16[57344]{0:T(1024)(128)(2,1)S(1)} %fusion.175), channel_id=1, replica_groups=mesh['row'=8,'ta'=4] {'row'}, dimensions={0}, use_global_device_ids=true | all-gather | bytes 1032192 | tf_op jit(solution)/shard_map/all_gather | solution.py:77
  1029.5 31.9 %all_gather.13 = bf16[458752]{0:T(1024)(128)(2,1)S(1)} all-gather(bf16[57344]{0:T(1024)(128)(2,1)S(1)} %fusion.174), channel_id=1, replica_groups=mesh['row'=8,'ta'=4] {'row'}, dimensions={0}, use_global_device_ids=true | all-gather | bytes 1032192 | tf_op jit(solution)/shard_map/all_gather | solution.py:78
  (393 shorter events, 365.3 us)
Async XLA Ops:
  11.0 83.2 %copy-start.14 = (bf16[1,256,896]{2,1,0:T(8,128)(2,1)S(1)}, bf16[1,256,896]{2,1,0:T(8,128)(2,1)}, u32[]{:S(2)}) copy-start(bf16[1,256,896]{2,1,0:T(8,128)(2,1)} %param.23) | copy-start | bytes 1376260
  11.1 38.7 %all-reduce.17.cloned.1.call-start = ((), (), s32[]{:S(2)}) async-start(), calls=%async_computation.1 | async-start | bytes 524288 | tf_op jit(solution)/shard_map/while/body/eval_jaxpr/psum | solution.py:30
  54.0 36.0 %all-reduce.17.cloned.1.call-start = ((), (), s32[]{:S(2)}) async-start(), calls=%async_computation.1 | async-start | bytes 524288 | tf_op jit(solution)/shard_map/while/body/eval_jaxpr/psum | solution.py:30
  98.1 34.9 %all-reduce.19.cloned.1.call-start = ((), (), s32[]{:S(2)}) async-start(), calls=%async_computation.2 | async-start | bytes 262144 | tf_op jit(solution)/shard_map/while/body/eval_jaxpr/psum | solution.py:45
  133.0 4.2 copy-start.40
  138.3 34.6 %all-reduce.19.cloned.1.call-start = ((), (), s32[]{:S(2)}) async-start(), calls=%async_computation.2 | async-start | bytes 262144 | tf_op jit(solution)/shard_map/while/body/eval_jaxpr/psum | solution.py:45
  179.2 35.1 %all-reduce.21.cloned.1.call-start = ((), (), s32[]{:S(2)}) async-start(), calls=%async_computation.3 | async-start | bytes 524288 | tf_op jit(solution)/shard_map/while/body/eval_jaxpr/psum | solution.py:30
  217.8 35.1 %all-reduce.21.cloned.1.call-start = ((), (), s32[]{:S(2)}) async-start(), calls=%async_computation.3 | async-start | bytes 524288 | tf_op jit(solution)/shard_map/while/body/eval_jaxpr/psum | solution.py:30
  263.1 34.9 %all-reduce.23.cloned.1.call-start = ((), (), s32[]{:S(2)}) async-start(), calls=%async_computation.4 | async-start | bytes 262144 | tf_op jit(solution)/shard_map/while/body/eval_jaxpr/psum | solution.py:45
  303.3 34.9 %all-reduce.23.cloned.1.call-start = ((), (), s32[]{:S(2)}) async-start(), calls=%async_computation.4 | async-start | bytes 262144 | tf_op jit(solution)/shard_map/while/body/eval_jaxpr/psum | solution.py:45
  344.5 78.8 %copy-start.15 = (bf16[1,256,896]{2,1,0:T(8,128)(2,1)S(1)}, bf16[1,256,896]{2,1,0:T(8,128)(2,1)}, u32[]{:S(2)}) copy-start(bf16[1,256,896]{2,1,0:T(8,128)(2,1)} %param.23) | copy-start | bytes 1376260
  344.6 36.0 %all-reduce.25.cloned.1.call-start = ((), (), s32[]{:S(2)}) async-start(), calls=%async_computation.5 | async-start | bytes 524288 | tf_op jit(solution)/shard_map/while/body/eval_jaxpr/psum | solution.py:30
  344.6 38.0 %copy-start = (bf16[2,256,896]{2,1,0:T(8,128)(2,1)S(1)}, bf16[2,256,896]{2,1,0:T(8,128)(2,1)}, u32[]{:S(2)}) copy-start(bf16[2,256,896]{2,1,0:T(8,128)(2,1)} %get-tuple-element.2377) | copy-start | bytes 2752516 | tf_op jit(solution)/shard_map/while
  384.1 35.7 %all-reduce.25.cloned.1.call-start = ((), (), s32[]{:S(2)}) async-start(), calls=%async_computation.5 | async-start | bytes 524288 | tf_op jit(solution)/shard_map/while/body/eval_jaxpr/psum | solution.py:30
  384.1 37.7 %copy-start = (bf16[2,256,896]{2,1,0:T(8,128)(2,1)S(1)}, bf16[2,256,896]{2,1,0:T(8,128)(2,1)}, u32[]{:S(2)}) copy-start(bf16[2,256,896]{2,1,0:T(8,128)(2,1)} %get-tuple-element.2377) | copy-start | bytes 2752516 | tf_op jit(solution)/shard_map/while
  428.8 34.9 %all-reduce.27.cloned.1.call-start = ((), (), s32[]{:S(2)}) async-start(), calls=%async_computation.6 | async-start | bytes 262144 | tf_op jit(solution)/shard_map/while/body/eval_jaxpr/psum | solution.py:45
  469.0 34.6 %all-reduce.27.cloned.1.call-start = ((), (), s32[]{:S(2)}) async-start(), calls=%async_computation.6 | async-start | bytes 262144 | tf_op jit(solution)/shard_map/while/body/eval_jaxpr/psum | solution.py:45
  509.9 35.5 %all-reduce.29.cloned.1.call-start = ((), (), s32[]{:S(2)}) async-start(), calls=%async_computation.7 | async-start | bytes 524288 | tf_op jit(solution)/shard_map/while/body/eval_jaxpr/psum | solution.py:30
  510.0 37.4 %copy-start.2 = (bf16[2,256,896]{2,1,0:T(8,128)(2,1)S(1)}, bf16[2,256,896]{2,1,0:T(8,128)(2,1)}, u32[]{:S(2)}) copy-start(bf16[2,256,896]{2,1,0:T(8,128)(2,1)} %get-tuple-element.2449) | copy-start | bytes 2752516 | tf_op jit(solution)/shard_map/while
  548.9 35.1 %all-reduce.29.cloned.1.call-start = ((), (), s32[]{:S(2)}) async-start(), calls=%async_computation.7 | async-start | bytes 524288 | tf_op jit(solution)/shard_map/while/body/eval_jaxpr/psum | solution.py:30
  548.9 37.1 %copy-start.2 = (bf16[2,256,896]{2,1,0:T(8,128)(2,1)S(1)}, bf16[2,256,896]{2,1,0:T(8,128)(2,1)}, u32[]{:S(2)}) copy-start(bf16[2,256,896]{2,1,0:T(8,128)(2,1)} %get-tuple-element.2449) | copy-start | bytes 2752516 | tf_op jit(solution)/shard_map/while
  593.0 35.2 %all-reduce.31.cloned.1.call-start = ((), (), s32[]{:S(2)}) async-start(), calls=%async_computation.8 | async-start | bytes 262144 | tf_op jit(solution)/shard_map/while/body/eval_jaxpr/psum | solution.py:45
  633.3 35.2 %all-reduce.31.cloned.1.call-start = ((), (), s32[]{:S(2)}) async-start(), calls=%async_computation.8 | async-start | bytes 262144 | tf_op jit(solution)/shard_map/while/body/eval_jaxpr/psum | solution.py:45
  673.6 249.7 %all-reduce.15.cloned.1.call-start = ((), (), s32[]{:S(2)}) async-start(), calls=%async_computation | async-start | bytes 14680064
  (71 other events, 130.3 us)
Sparse Core Ops, SparseCore 0:
  14.8 34.9 all-reduce.16
  57.7 32.2 all-reduce.16
  101.2 31.7 all-reduce.18
  141.1 31.7 all-reduce.18
  182.0 32.2 all-reduce.20
  220.7 32.2 all-reduce.20
  266.2 31.7 all-reduce.22
  306.4 31.7 all-reduce.22
  348.3 32.2 all-reduce.24
  387.5 32.2 all-reduce.24
  431.9 31.7 all-reduce.26
  471.7 31.7 all-reduce.26
  513.1 32.2 all-reduce.28
  551.7 32.2 all-reduce.28
  596.4 31.7 all-reduce.30
  636.7 31.7 all-reduce.30
Sparse Core Ops, SparseCore 1:
  684.2 239.1 all-reduce.14
where the time goes:
time: 1070 us
  waiting for transfers between devices  691 us (65%)
  blocking collectives  178 us (17%)
  matrix products  85.7 us (8%)
  local copies, waits for them, and re-layouts  72.1 us (7%)
  other arithmetic  26.6 us (2%)
  between operations  16.1 us (2%)
    psum x8, waiting for transfers between devices, backward_layer(): lax.psum((contract(grad_low, w_up, 1, 1) * RANK ** (-0.5)).astype(jnp.bfl...  240 us
    unnamed x2, waiting for transfers between devices  237 us
    psum x8, waiting for transfers between devices, forward_layer(): projected, total_sq = lax.psum((partial_value, squares), 'ta')  213 us
    dot_general x32, matrix products, contract(): lax.dot_general(matrix_a, matrix_b, (((dim_a,), (dim_b,)), ((), ())), pre...  57 us
    psum x8, blocking collectives, forward_layer(): projected, total_sq = lax.psum((partial_value, squares), 'ta')  48.4 us
    all_gather x1, blocking collectives, average_whole(): lax.all_gather(share_down, 'row', axis=0, tiled=True)  32.7 us
    all_gather x1, blocking collectives, average_whole(): lax.all_gather((totals[2] / replicas).astype(jnp.bfloat16), 'row', axis=0...  32.4 us
    all_gather x1, blocking collectives, average_whole(): lax.all_gather((totals[3] / replicas).astype(jnp.bfloat16), 'row', axis=0...  32.4 us
  transfers between devices with their start and end apart: 17, of which 17 were waited for; matrix products, arithmetic and copies ran while one was open for 3% of the time, Pallas kernels for 0%

commit v1 on v0

--- a/solution.py
+++ b/solution.py
@@ -42,8 +42,12 @@
     w_down, w_up = weights
     grad_low = gradient.astype(jnp.bfloat16)
     grad_up = contract(activation, grad_low, 0, 0) * RANK ** (-0.5)
-    grad_act = lax.psum(
-        (contract(grad_low, w_up, 1, 1) * RANK ** (-0.5)).astype(jnp.bfloat16), "ta"
+
+    def see_domain_all(local):
+        return lax.all_gather(local, axis_name="ta").sum(axis=0)
+
+    grad_act = see_domain_all(
+        (contract(grad_low, w_up, 1, 1) * RANK ** (-0.5)).astype(jnp.bfloat16)
     ).astype(jnp.float32)
     grad_pre = grad_act * silu_slope(preact)
     row_dot = jnp.sum(grad_pre * preact, axis=1, keepdims=True)

time: 1070 us -> 906 us (0.85)
  waiting for transfers between devices: 691 us -> 450 us
  blocking collectives: 178 us -> 237 us
  local copies, waits for them, and re-layouts: 72.1 us -> 96.8 us
  matrix products: 85.7 us -> 67.2 us
    psum x8 -> x0, waiting for transfers between devices: 240 us -> none  [backward_layer(): lax.psum((contract(grad_low, w_up, 1, 1) * RANK ** (-0.5)).astype(jnp.bfl...]
    all_gather x0 -> x8, blocking collectives: none -> 56 us  [see_domain_all(): return lax.all_gather(local, axis_name='ta').sum(axis=0)]
    while x132 -> x192, local copies, waits for them, and re-layouts: 21.4 us -> 41.3 us
    dot_general x32, matrix products: 57 us -> 38.4 us  [contract(): lax.dot_general(matrix_a, matrix_b, (((dim_a,), (dim_b,)), ((), ())), pre...]
  transfers between devices with their start and end apart: 17 -> 9, of which waited for: 17 -> 9; matrix products, arithmetic and copies ran while one was open for 3% -> 1% of each run, Pallas kernels for 0% -> 0%
where the time goes in v1:
time: 906 us; the launch traced here: 904 us
  waiting for transfers between devices  450 us (50%)
  blocking collectives  237 us (26%)
  local copies, waits for them, and re-layouts  96.8 us (11%)
  matrix products  67.2 us (7%)
  other arithmetic  33.6 us (4%)
  between operations  16.4 us (2%)
    unnamed x2, waiting for transfers between devices  238 us
    psum x8, waiting for transfers between devices, forward_layer(): projected, total_sq = lax.psum((partial_value, squares), 'ta')  212 us
    all_gather x8, blocking collectives, see_domain_all(): return lax.all_gather(local, axis_name='ta').sum(axis=0)  56 us
    psum x8, blocking collectives, forward_layer(): projected, total_sq = lax.psum((partial_value, squares), 'ta')  51.6 us
    while x192, local copies, waits for them, and re-layouts  41.3 us
    dot_general x32, matrix products, contract(): lax.dot_general(matrix_a, matrix_b, (((dim_a,), (dim_b,)), ((), ())), pre...  38.4 us
    all_gather x1, blocking collectives, average_whole(): lax.all_gather(share_down, 'row', axis=0, tiled=True)  32.7 us
    all_gather x1, blocking collectives, average_whole(): lax.all_gather((totals[2] / replicas).astype(jnp.bfloat16), 'row', axis=0...  32.4 us
  transfers between devices with their start and end apart: 9, of which 9 were waited for; matrix products, arithmetic and copies ran while one was open for 1% of the time, Pallas kernels for 0%

profile of v1, /device:TPU:0, one launch (start us, length us, event | category | flops | bytes accessed | tf_op | source)
XLA Modules:
  0.0 903.5 jit_solution(3164992369464395191)
XLA Ops:
  11.0 83.1 %while.160 = (s32[]{:T(128)}, bf16[256,896]{1,0:T(8,128)(2,1)S(1)}, bf16[2,256,896]{2,1,0:T(8,128)(2,1)}, f32[2,256,1]{1,2,0:T(1,128)S(1)}, f32[2,256,256]{1,2,0...) while((s32[]{:T(128)}, bf16[256,896]{1,0:T(8,128)(2,1)S(1)}, ...), condition=%wide.region_4.5_spmd, body=%wide.region_0.4_spmd.sunk | while | flops 237470208 | bytes 6695077 | solution.py:105
  14.2 8.3 psum.65
  22.6 27.2 %all-reduce.13.cloned.1.call-done = f32[256,256]{0,1:T(8,128)} async-done(((f32[256,256]{0,1:T(8,128)}), f32[256,256]{0,1:T(8,128)}) %all-reduce.13.cloned.1.call-update) | async-done | bytes 262160 | tf_op jit(solution)/shard_map/while/body/eval_jaxpr/psum | solution.py:30
  62.8 27.1 %all-reduce.13.cloned.1.call-done = f32[256,256]{0,1:T(8,128)} async-done(((f32[256,256]{0,1:T(8,128)}), f32[256,256]{0,1:T(8,128)}) %all-reduce.13.cloned.1.call-update) | async-done | bytes 262160 | tf_op jit(solution)/shard_map/while/body/eval_jaxpr/psum | solution.py:30
  99.0 40.9 %while.161 = (s32[]{:T(128)}, f32[256,896]{1,0:T(8,128)S(1)}, bf16[2,896,256]{2,1,0:T(8,128)(2,1)}, bf16[2,256,896]{2,1,0:T(8,128)(2,1)}, f32[2,896,256]{2,1,0:T...) while((s32[]{:T(128)}, f32[256,896]{1,0:T(8,128)S(1)}, ...), condition=%wide.region_8.9_spmd, body=%wide.region_5.8_spmd.sunk | while | flops 477298944 | bytes 75642352 | solution.py:107
  120.4 7.7 all-gather.8
  141.0 78.3 %while.162 = (s32[]{:T(128)}, bf16[256,896]{1,0:T(8,128)(2,1)S(1)}, bf16[2,256,896]{2,1,0:T(8,128)(2,1)}, f32[2,256,1]{1,2,0:T(1,128)S(1)}, f32[2,256,256]{1,2,0...) while((s32[]{:T(128)}, bf16[256,896]{1,0:T(8,128)(2,1)S(1)}, ...), condition=%wide.region_13.14_spmd, body=%wide.region_9.13_spmd.sunk | while | flops 237470208 | bytes 10365121 | solution.py:105
  151.1 26.1 %all-reduce.15.cloned.1.call-done = f32[256,256]{0,1:T(8,128)} async-done(((f32[256,256]{0,1:T(8,128)}), f32[256,256]{0,1:T(8,128)}) %all-reduce.15.cloned.1.call-update) | async-done | bytes 262160 | tf_op jit(solution)/shard_map/while/body/eval_jaxpr/psum | solution.py:30
  189.6 26.2 %all-reduce.15.cloned.1.call-done = f32[256,256]{0,1:T(8,128)} async-done(((f32[256,256]{0,1:T(8,128)}), f32[256,256]{0,1:T(8,128)}) %all-reduce.15.cloned.1.call-update) | async-done | bytes 262160 | tf_op jit(solution)/shard_map/while/body/eval_jaxpr/psum | solution.py:30
  224.8 37.3 %while.163 = (s32[]{:T(128)}, f32[256,896]{1,0:T(8,128)S(1)}, bf16[2,896,256]{2,1,0:T(8,128)(2,1)}, bf16[2,256,896]{2,1,0:T(8,128)(2,1)}, f32[2,896,256]{2,1,0:T...) while((s32[]{:T(128)}, f32[256,896]{1,0:T(8,128)S(1)}, ...), condition=%wide.region_17.18_spmd, body=%wide.region_14.17_spmd.sunk | while | flops 477298944 | bytes 77739560 | solution.py:107
  263.2 79.3 %while.164 = (s32[]{:T(128)}, bf16[256,896]{1,0:T(8,128)(2,1)S(1)}, bf16[2,256,896]{2,1,0:T(8,128)(2,1)}, f32[2,256,1]{1,2,0:T(1,128)S(1)}, f32[2,256,256]{1,2,0...) while((s32[]{:T(128)}, bf16[256,896]{1,0:T(8,128)(2,1)S(1)}, ...), condition=%wide.region_22.23_spmd, body=%wide.region_18.22_spmd.sunk | while | flops 237470208 | bytes 10365121 | solution.py:105
  273.4 26.4 %all-reduce.17.cloned.1.call-done = f32[256,256]{0,1:T(8,128)} async-done(((f32[256,256]{0,1:T(8,128)}), f32[256,256]{0,1:T(8,128)}) %all-reduce.17.cloned.1.call-update) | async-done | bytes 262160 | tf_op jit(solution)/shard_map/while/body/eval_jaxpr/psum | solution.py:30
  312.3 26.7 %all-reduce.17.cloned.1.call-done = f32[256,256]{0,1:T(8,128)} async-done(((f32[256,256]{0,1:T(8,128)}), f32[256,256]{0,1:T(8,128)}) %all-reduce.17.cloned.1.call-update) | async-done | bytes 262160 | tf_op jit(solution)/shard_map/while/body/eval_jaxpr/psum | solution.py:30
  347.9 35.7 %while.165 = (s32[]{:T(128)}, f32[256,896]{1,0:T(8,128)S(1)}, bf16[2,896,256]{2,1,0:T(8,128)(2,1)}, bf16[2,256,896]{2,1,0:T(8,128)(2,1)}, f32[2,896,256]{2,1,0:T...) while((s32[]{:T(128)}, f32[256,896]{1,0:T(8,128)S(1)}, ...), condition=%wide.region_26.27_spmd, body=%wide.region_23.26_spmd.sunk | while | flops 477298944 | bytes 73545176 | solution.py:107
  384.7 78.6 %while.166 = (s32[]{:T(128)}, bf16[256,896]{1,0:T(8,128)(2,1)S(1)}, bf16[2,256,896]{2,1,0:T(8,128)(2,1)}, f32[2,256,1]{1,2,0:T(1,128)S(1)}, f32[2,256,256]{1,2,0...) while((s32[]{:T(128)}, bf16[256,896]{1,0:T(8,128)(2,1)S(1)}, ...), condition=%wide.region_31.32_spmd, body=%wide.region_27.31_spmd.sunk | while | flops 237470208 | bytes 10365121 | solution.py:105
  394.7 26.1 %all-reduce.19.cloned.1.call-done = f32[256,256]{0,1:T(8,128)} async-done(((f32[256,256]{0,1:T(8,128)}), f32[256,256]{0,1:T(8,128)}) %all-reduce.19.cloned.1.call-update) | async-done | bytes 262160 | tf_op jit(solution)/shard_map/while/body/eval_jaxpr/psum | solution.py:30
  433.2 26.5 %all-reduce.19.cloned.1.call-done = f32[256,256]{0,1:T(8,128)} async-done(((f32[256,256]{0,1:T(8,128)}), f32[256,256]{0,1:T(8,128)}) %all-reduce.19.cloned.1.call-update) | async-done | bytes 262160 | tf_op jit(solution)/shard_map/while/body/eval_jaxpr/psum | solution.py:30
  468.8 38.2 %while.167 = (s32[]{:T(128)}, f32[256,896]{1,0:T(8,128)S(1)}, bf16[2,896,256]{2,1,0:T(8,128)(2,1)}, bf16[2,256,896]{2,1,0:T(8,128)(2,1)}, f32[2,896,256]{2,1,0:T...) while((s32[]{:T(128)}, f32[256,896]{1,0:T(8,128)S(1)}, ...), condition=%wide.region_35.36_spmd, body=%wide.region_32.35_spmd.sunk | while | flops 477298944 | bytes 74069488 | solution.py:107
  488.6 7.3 all-gather.11
  518.2 238.0 %all-reduce.11.cloned.1.call-done = (f32[458752]{0:T(1024)}, f32[458752]{0:T(1024)}, f32[458752]{0:T(1024)}, f32[458752]{0:T(1024)}) async-done(((f32[458752]{0:T(1024)}, f32[458752]{0:T(1024)}, f32[458752]{0:T(1024)}, f32[458752]{0:T(1024)}), (f32[458752]{0:T(1024)}, f32[458752]{0:T(1024)}, f32[458752]{0:T(1024)}, f32[458752]{0:T(1024)})) %all-reduce.11.cloned.1.call-update) | async-done | bytes 7340048
  757.2 32.4 %all_gather.86 = bf16[458752]{0:T(1024)(128)(2,1)S(1)} all-gather(bf16[57344]{0:T(1024)(128)(2,1)S(1)} %fusion.193), channel_id=1, replica_groups=mesh['row'=8,'ta'=4] {'row'}, dimensions={0}, use_global_device_ids=true | all-gather | bytes 1032192 | tf_op jit(solution)/shard_map/all_gather | solution.py:85
  792.0 32.4 %all_gather.87 = bf16[458752]{0:T(1024)(128)(2,1)S(1)} all-gather(bf16[57344]{0:T(1024)(128)(2,1)S(1)} %fusion.192), channel_id=1, replica_groups=mesh['row'=8,'ta'=4] {'row'}, dimensions={0}, use_global_device_ids=true | all-gather | bytes 1032192 | tf_op jit(solution)/shard_map/all_gather | solution.py:88
  827.4 32.7 %all_gather.84 = bf16[458752]{0:T(1024)(128)(2,1)S(1)} all-gather(bf16[57344]{0:T(1024)(128)(2,1)S(1)} %fusion.195), channel_id=1, replica_groups=mesh['row'=8,'ta'=4] {'row'}, dimensions={0}, use_global_device_ids=true | all-gather | bytes 1032192 | tf_op jit(solution)/shard_map/all_gather | solution.py:81
  862.4 31.9 %all_gather.85 = bf16[458752]{0:T(1024)(128)(2,1)S(1)} all-gather(bf16[57344]{0:T(1024)(128)(2,1)S(1)} %fusion.194), channel_id=1, replica_groups=mesh['row'=8,'ta'=4] {'row'}, dimensions={0}, use_global_device_ids=true | all-gather | bytes 1032192 | tf_op jit(solution)/shard_map/all_gather | solution.py:82
  (463 shorter events, 282.4 us)
Async XLA Ops:
  11.0 83.2 %copy-start.29 = (bf16[1,256,896]{2,1,0:T(8,128)(2,1)S(1)}, bf16[1,256,896]{2,1,0:T(8,128)(2,1)}, u32[]{:S(2)}) copy-start(bf16[1,256,896]{2,1,0:T(8,128)(2,1)} %param.23) | copy-start | bytes 1376260
  11.0 38.7 %all-reduce.13.cloned.1.call-start = ((), (), s32[]{:S(2)}) async-start(), calls=%async_computation.1 | async-start | bytes 524288 | tf_op jit(solution)/shard_map/while/body/eval_jaxpr/psum | solution.py:30
  54.0 36.0 %all-reduce.13.cloned.1.call-start = ((), (), s32[]{:S(2)}) async-start(), calls=%async_computation.1 | async-start | bytes 524288 | tf_op jit(solution)/shard_map/while/body/eval_jaxpr/psum | solution.py:30
  109.5 4.3 copy-start.25
  130.3 4.3 copy-start.25
  141.0 78.3 %copy-start.30 = (bf16[1,256,896]{2,1,0:T(8,128)(2,1)S(1)}, bf16[1,256,896]{2,1,0:T(8,128)(2,1)}, u32[]{:S(2)}) copy-start(bf16[1,256,896]{2,1,0:T(8,128)(2,1)} %param.23) | copy-start | bytes 1376260
  141.0 36.1 %all-reduce.15.cloned.1.call-start = ((), (), s32[]{:S(2)}) async-start(), calls=%async_computation.2 | async-start | bytes 524288 | tf_op jit(solution)/shard_map/while/body/eval_jaxpr/psum | solution.py:30
  141.0 38.1 %copy-start.2 = (bf16[2,256,896]{2,1,0:T(8,128)(2,1)S(1)}, bf16[2,256,896]{2,1,0:T(8,128)(2,1)}, u32[]{:S(2)}) copy-start(bf16[2,256,896]{2,1,0:T(8,128)(2,1)} %get-tuple-element.2312) | copy-start | bytes 2752516 | tf_op jit(solution)/shard_map/while
  180.6 35.1 %all-reduce.15.cloned.1.call-start = ((), (), s32[]{:S(2)}) async-start(), calls=%async_computation.2 | async-start | bytes 524288 | tf_op jit(solution)/shard_map/while/body/eval_jaxpr/psum | solution.py:30
  180.7 37.1 %copy-start.2 = (bf16[2,256,896]{2,1,0:T(8,128)(2,1)S(1)}, bf16[2,256,896]{2,1,0:T(8,128)(2,1)}, u32[]{:S(2)}) copy-start(bf16[2,256,896]{2,1,0:T(8,128)(2,1)} %get-tuple-element.2312) | copy-start | bytes 2752516 | tf_op jit(solution)/shard_map/while
  263.2 79.3 %copy-start.31 = (bf16[1,256,896]{2,1,0:T(8,128)(2,1)S(1)}, bf16[1,256,896]{2,1,0:T(8,128)(2,1)}, u32[]{:S(2)}) copy-start(bf16[1,256,896]{2,1,0:T(8,128)(2,1)} %param.23) | copy-start | bytes 1376260
  263.4 36.4 %all-reduce.17.cloned.1.call-start = ((), (), s32[]{:S(2)}) async-start(), calls=%async_computation.3 | async-start | bytes 524288 | tf_op jit(solution)/shard_map/while/body/eval_jaxpr/psum | solution.py:30
  263.4 38.4 %copy-start.7 = (bf16[2,256,896]{2,1,0:T(8,128)(2,1)S(1)}, bf16[2,256,896]{2,1,0:T(8,128)(2,1)}, u32[]{:S(2)}) copy-start(bf16[2,256,896]{2,1,0:T(8,128)(2,1)} %get-tuple-element.2387) | copy-start | bytes 2752516 | tf_op jit(solution)/shard_map/while
  303.3 35.7 %all-reduce.17.cloned.1.call-start = ((), (), s32[]{:S(2)}) async-start(), calls=%async_computation.3 | async-start | bytes 524288 | tf_op jit(solution)/shard_map/while/body/eval_jaxpr/psum | solution.py:30
  303.3 37.7 %copy-start.7 = (bf16[2,256,896]{2,1,0:T(8,128)(2,1)S(1)}, bf16[2,256,896]{2,1,0:T(8,128)(2,1)}, u32[]{:S(2)}) copy-start(bf16[2,256,896]{2,1,0:T(8,128)(2,1)} %get-tuple-element.2387) | copy-start | bytes 2752516 | tf_op jit(solution)/shard_map/while
  374.1 4.2 copy-start.21
  384.7 79.3 %copy-start.32 = (bf16[1,256,896]{2,1,0:T(8,128)(2,1)S(1)}, bf16[1,256,896]{2,1,0:T(8,128)(2,1)}, u32[]{:S(2)}) copy-start(bf16[1,256,896]{2,1,0:T(8,128)(2,1)} %param.23) | copy-start | bytes 1376260
  384.7 36.1 %all-reduce.19.cloned.1.call-start = ((), (), s32[]{:S(2)}) async-start(), calls=%async_computation.4 | async-start | bytes 524288 | tf_op jit(solution)/shard_map/while/body/eval_jaxpr/psum | solution.py:30
  384.7 38.1 %copy-start.12 = (bf16[2,256,896]{2,1,0:T(8,128)(2,1)S(1)}, bf16[2,256,896]{2,1,0:T(8,128)(2,1)}, u32[]{:S(2)}) copy-start(bf16[2,256,896]{2,1,0:T(8,128)(2,1)} %get-tuple-element.2462) | copy-start | bytes 2752516 | tf_op jit(solution)/shard_map/while
  424.3 35.5 %all-reduce.19.cloned.1.call-start = ((), (), s32[]{:S(2)}) async-start(), calls=%async_computation.4 | async-start | bytes 524288 | tf_op jit(solution)/shard_map/while/body/eval_jaxpr/psum | solution.py:30
  424.3 37.4 %copy-start.12 = (bf16[2,256,896]{2,1,0:T(8,128)(2,1)S(1)}, bf16[2,256,896]{2,1,0:T(8,128)(2,1)}, u32[]{:S(2)}) copy-start(bf16[2,256,896]{2,1,0:T(8,128)(2,1)} %get-tuple-element.2462) | copy-start | bytes 2752516 | tf_op jit(solution)/shard_map/while
  463.2 293.0 %all-reduce.11.cloned.1.call-start = ((), (), s32[]{:S(2)}) async-start(), calls=%async_computation | async-start | bytes 14680064
  477.5 4.5 copy-start.45
  497.0 4.4 copy-start.45
  (98 other events, 189.2 us)
Sparse Core Ops, SparseCore 0:
  14.8 34.9 all-reduce.12
  57.7 32.2 all-reduce.12
  144.1 32.9 all-reduce.14
  183.5 32.2 all-reduce.14
  266.8 32.9 all-reduce.16
  306.7 32.2 all-reduce.16
  387.8 32.8 all-reduce.18
  427.4 32.2 all-reduce.18
Sparse Core Ops, SparseCore 1:
  516.4 239.7 all-reduce.10
